TPU v7x, 32 devices: a whole 2x2x4 slice. The times are simulated.
32 devices in a mesh: expert: 2 (over x), batch: 4 (over z), seq: 4 (over y, core).
Axes of the slice: x: 2, y: 2, z: 4, core: 2. Of those that a mesh axis runs over, the one named last changes fastest.
Arguments:
- queries: bfloat16 [2, 4, 2, 384, 4096], P('expert', 'batch', None, 'seq'), may hold values from -36 to 36
- keys: bfloat16 [2, 4, 2, 384, 4096], P('expert', 'batch', None, 'seq'), may hold values from -21 to 21
- values: bfloat16 [2, 4, 2, 384, 4096], P('expert', 'batch', None, 'seq'), may hold values from -6 to 6
- latents: bfloat16 [2, 4, 384, 4096], P('expert', 'batch', 'seq'), may hold values from -6 to 6
- gain: bfloat16 [2, 4096], P('expert'), may hold values from 0.099609375 to 1.8984375
- steps_table: int32 [2, 4], P('expert', 'batch'), may hold values from 0 to 38
- flags: int32 [4], P('batch'), may hold values 0 or 1
Outputs:
- denoised: bfloat16 [2, 4, 384, 4096], P('expert', 'batch', 'seq')
- next_latents: bfloat16 [2, 4, 384, 4096], P('expert', 'batch', 'seq')
All inputs are finite; a program needn't handle non-finite values. No bound on the sum of `flags` on one device may be relied on, other than what follows from the above.
Results may differ from a plain program's by a relative error of at most 0.006.
Values may be sent and summed in bfloat16 or wider, within the bound.
A program may use at most 64 MiB of HBM per device.

v0:
```python
import jax
import jax.numpy as jnp
from jax import lax
from jax.sharding import PartitionSpec as P

HDIM = 128
STEPS = 40


GUIDANCE = 3.5
flow_shift = 5.0


def from_partner(block, axis, bit):
    count = lax.axis_size(axis)
    route = []
    for low in range(count):
        high = low | 1 << bit
        if high != low and high < count:
            route += [(low, high), (high, low)]
    return lax.ppermute(block, axis, route)


def sigma_of(step):
    level = 1.0 - step.astype(jnp.float32) / STEPS
    return flow_shift * level / (1.0 + (flow_shift - 1.0) * level)


def combine(cond, uncond):
    base = uncond.astype(jnp.float32)
    return (base + GUIDANCE * (cond.astype(jnp.float32) - base)).astype(jnp.bfloat16)


def attend(stacked):
    query_heads, key_heads, value_heads = stacked
    items, length, width_dev = query_heads.shape
    heads_dev = width_dev // HDIM
    block = 512 if length % 512 == 0 else length
    key_rows = key_heads.reshape(items, length, heads_dev, HDIM)
    value_rows = value_heads.reshape(items, length, heads_dev, HDIM)
    query_blocks = query_heads.reshape(items, length // block, block, heads_dev, HDIM).transpose(
        1, 0, 2, 3, 4
    )

    def one_block(query_part):
        scores = jnp.einsum(
            "nqhd,nkhd->nhqk", query_part, key_rows, preferred_element_type=jnp.float32
        ) * HDIM ** (-0.5)
        weights = jax.nn.softmax(scores, axis=-1).astype(jnp.bfloat16)
        return jnp.einsum(
            "nhqk,nkhd->nqhd", weights, value_rows, preferred_element_type=jnp.float32
        ).astype(jnp.bfloat16)

    result = lax.map(one_block, query_blocks)
    return result.transpose(1, 0, 2, 3, 4).reshape(items, length, width_dev)


def per_device(queries, keys, values, latents, gain, steps_table, flags):
    attended = attend(
        (
            lax.all_to_all(queries[0, 0], "seq", split_axis=2, concat_axis=1, tiled=True),
            lax.all_to_all(keys[0, 0], "seq", split_axis=2, concat_axis=1, tiled=True),
            lax.all_to_all(values[0, 0], "seq", split_axis=2, concat_axis=1, tiled=True),
        )
    )
    guided = lax.all_to_all(
        combine(attended[0], attended[1]), "seq", split_axis=0, concat_axis=1, tiled=True
    )
    guided_f32 = guided.astype(jnp.float32)
    scale = lax.rsqrt(jnp.mean(guided_f32 * guided_f32, axis=-1, keepdims=True) + 1e-06)
    velocity = guided_f32 * scale * gain[0].astype(jnp.float32)[None, :]
    step_now = steps_table[0, 0]
    sigma_now = sigma_of(step_now)
    sigma_next = sigma_of(step_now + 1)
    current = latents[0, 0].astype(jnp.float32)
    denoised = (current - sigma_now * velocity).astype(jnp.bfloat16)
    moved = (current + (sigma_next - sigma_now) * velocity).astype(jnp.bfloat16)
    partner = from_partner(moved, "expert", 0)
    next_latents = jnp.where(flags[0] == 1, partner, moved)
    return (denoised[None, None], next_latents[None, None])


def solution(mesh):
    placed = (
        P("expert", "batch", None, "seq", None),
        P("expert", "batch", None, "seq", None),
        P("expert", "batch", None, "seq", None),
        P("expert", "batch", "seq", None),
        P("expert", None),
        P("expert", "batch"),
        P("batch"),
    )
    return jax.shard_map(
        per_device,
        mesh=mesh,
        in_specs=placed,
        out_specs=(P("expert", "batch", "seq", None), P("expert", "batch", "seq", None)),
        check_vma=False,
    )
```

profile of v0, /device:TPU:0, one launch (start us, length us, event | category | flops | bytes accessed | tf_op | source)
XLA Modules:
  0.0 159.6 jit_solution(14842761862056379476)
XLA Ops:
  0.6 5.7 %copy.30 = bf16[1,1,2,96,4096]{3,2,4,1,0:T(2,128)(2,1)} copy(bf16[1,1,2,96,4096]{4,3,2,1,0:T(8,128)(2,1)} %param.7) | data formatting | bytes 3145728 | tf_op args[0]
  6.3 4.3 %all-to-all-start = ((bf16[2,96,4096]{1,0,2:T(2,128)(2,1)}), bf16[2,96,4096]{1,0,2:T(2,128)(2,1)S(1)}, u32[]{:S(2)}, u32[]{:S(2)}) async-start(bf16[2,96,4096]{1,0,2:T(2,128)(2,1)} %bitcast.50), calls=%async_computation | async-start | bytes 4194304 | tf_op jit(solution)/shard_map/all_to_all | solution.py:61
  10.6 5.7 %copy.32 = bf16[1,1,2,96,4096]{3,2,4,1,0:T(2,128)(2,1)} copy(bf16[1,1,2,96,4096]{4,3,2,1,0:T(8,128)(2,1)} %param.8) | data formatting | bytes 3145728 | tf_op args[1]
  16.3 20.0 %all-to-all-done = bf16[2,96,4096]{1,0,2:T(2,128)(2,1)S(1)} async-done(((bf16[2,96,4096]{1,0,2:T(2,128)(2,1)}), bf16[2,96,4096]{1,0,2:T(2,128)(2,1)S(1)}, u32[]{:S(2)}, u32[]{:S(2)}) %all-to-all-start) | async-done | bytes 1572896 | tf_op jit(solution)/shard_map/all_to_all | solution.py:61
  36.3 4.4 %all-to-all-start.1 = ((bf16[2,96,4096]{1,0,2:T(2,128)(2,1)}), bf16[2,96,4096]{1,0,2:T(2,128)(2,1)}, u32[]{:S(2)}, u32[]{:S(2)}) async-start(bf16[2,96,4096]{1,0,2:T(2,128)(2,1)} %bitcast.49), calls=%async_computation.1 | async-start | bytes 4194304 | tf_op jit(solution)/shard_map/all_to_all | solution.py:62
  40.7 5.7 %copy.36 = bf16[1,1,2,96,4096]{3,2,4,1,0:T(2,128)(2,1)} copy(bf16[1,1,2,96,4096]{4,3,2,1,0:T(8,128)(2,1)} %param.9) | data formatting | bytes 3145728 | tf_op args[2]
  46.4 20.0 %all-to-all-done.1 = bf16[2,96,4096]{1,0,2:T(2,128)(2,1)} async-done(((bf16[2,96,4096]{1,0,2:T(2,128)(2,1)}), bf16[2,96,4096]{1,0,2:T(2,128)(2,1)}, u32[]{:S(2)}, u32[]{:S(2)}) %all-to-all-start.1) | async-done | bytes 1572896 | tf_op jit(solution)/shard_map/all_to_all | solution.py:62
  66.4 4.4 %all-to-all-start.2 = ((bf16[2,96,4096]{1,0,2:T(2,128)(2,1)}), bf16[2,96,4096]{1,0,2:T(2,128)(2,1)}, u32[]{:S(2)}, u32[]{:S(2)}) async-start(bf16[2,96,4096]{1,0,2:T(2,128)(2,1)} %bitcast.48), calls=%async_computation.2 | async-start | bytes 4194304 | tf_op jit(solution)/shard_map/all_to_all | solution.py:63
  70.9 3.7 %copy.31 = bf16[2,96,4,1024]{3,1,2,0:T(8,128)(2,1)} copy(bf16[2,96,4,1024]{1,0,3,2:T(2,128)(2,1)S(1)} %bitcast.47) | data formatting | bytes 3145728 | tf_op jit(solution)/shard_map/all_to_all | solution.py:61
  74.6 1.8 %copy.46 = bf16[96,8,8,128]{3,2,1,0:T(8,128)(2,1)S(1)} copy(bf16[96,8,8,128]{3,1,2,0:T(8,128)(2,1)} %bitcast.54) | data formatting | bytes 3145728
  76.4 4.7 %copy.33 = bf16[2,96,4,1024]{3,1,2,0:T(8,128)(2,1)S(1)} copy(bf16[2,96,4,1024]{1,0,3,2:T(2,128)(2,1)} %bitcast.5) | data formatting | bytes 3145728 | tf_op jit(solution)/shard_map/all_to_all | solution.py:62
  83.0 3.6 %copy-done = f32[2,8,384,384]{2,3,1,0:T(8,128)} copy-done((f32[2,8,384,384]{2,3,1,0:T(8,128)}, f32[2,8,384,384]{2,3,1,0:T(8,128)S(1)}, u32[]{:S(2)}) %copy-start) | copy-done | bytes 9437208
  86.6 2.4 %fusion.26 = f32[2,8,384]{2,1,0:T(8,128)S(1)} fusion(f32[2,8,384,384]{2,3,1,0:T(8,128)S(1)} %fusion.12), kind=kOutput, calls=%fused_computation.30 | output fusion | flops 9437567 | bytes 9461760 | tf_op jit(solution)/shard_map/while/body/eval_jaxpr/sub | solution.py:49
  89.0 7.6 %all-to-all-done.2 = bf16[2,96,4096]{1,0,2:T(2,128)(2,1)} async-done(((bf16[2,96,4096]{1,0,2:T(2,128)(2,1)}), bf16[2,96,4096]{1,0,2:T(2,128)(2,1)}, u32[]{:S(2)}, u32[]{:S(2)}) %all-to-all-start.2) | async-done | bytes 1572896 | tf_op jit(solution)/shard_map/all_to_all | solution.py:63
  96.6 4.7 %copy.37 = bf16[2,96,4,1024]{3,1,2,0:T(8,128)(2,1)S(1)} copy(bf16[2,96,4,1024]{1,0,3,2:T(2,128)(2,1)} %bitcast.8) | data formatting | bytes 3145728 | tf_op jit(solution)/shard_map/all_to_all | solution.py:63
  101.7 9.9 %fusion.15 = bf16[2,384,8,128]{3,1,2,0:T(8,128)(2,1)S(1)} fusion(bf16[2,384,8,128]{3,2,1,0:T(8,128)(2,1)S(1)} %bitcast.57, f32[2,8,384]{2,1,0:T(8,128)S(1)} %fusion.26, f32[2,8,384,384]{2,3,1,0:T(8,128)} %copy-done), kind=kOutput, calls=%fused_computation.22 | convolution fusion | flops 616569216 | bytes 12607488 | tf_op jit(solution)/shard_map/while/body/eval_jaxpr/nhqk,nkhd->nqhd/dot_general | solution.py:50
  112.8 1.4 reshape.129
  117.0 2.6 %add_convert_fusion = bf16[4,96,1024]{2,1,0:T(8,128)(2,1)} fusion(f32[4,96,1024]{2,1,0:T(8,128)S(1)} %copy-done.1, f32[4,96,1024]{2,1,0:T(8,128)} %reshape.130), kind=kLoop, calls=%fused_computation.21 | loop fusion | flops 1572864 | bytes 3932160 | tf_op jit(solution)/shard_map/convert_element_type | solution.py:31
  119.7 3.8 %all-to-all-start.3 = ((bf16[4,96,1024]{2,1,0:T(8,128)(2,1)}), bf16[4,96,1024]{2,1,0:T(8,128)(2,1)S(1)}, u32[]{:S(2)}, u32[]{:S(2)}) async-start(bf16[4,96,1024]{2,1,0:T(8,128)(2,1)} %add_convert_fusion), calls=%async_computation.3 | async-start | bytes 1572864 | tf_op jit(solution)/shard_map/all_to_all | solution.py:66
  124.9 10.0 %all-to-all-done.3 = bf16[4,96,1024]{2,1,0:T(8,128)(2,1)S(1)} async-done(((bf16[4,96,1024]{2,1,0:T(8,128)(2,1)}), bf16[4,96,1024]{2,1,0:T(8,128)(2,1)S(1)}, u32[]{:S(2)}, u32[]{:S(2)}) %all-to-all-start.3) | async-done | bytes 786464 | tf_op jit(solution)/shard_map/all_to_all | solution.py:66
  137.7 2.3 %collective-permute-start = (bf16[96,4096]{1,0:T(8,128)(2,1)}, bf16[96,4096]{1,0:T(8,128)(2,1)}, u32[]{:S(2)}, u32[]{:S(2)}) collective-permute-start(bf16[96,4096]{1,0:T(8,128)(2,1)} %fusion.9), channel_id=1, source_target_pairs={{0,16},{16,0},{1,17},{17,1},{2,18},{18,2},{3,19},{19,3},{4,20},{20... | collective-permute-start | bytes 2359304 | tf_op jit(solution)/shard_map/ppermute | solution.py:21
  142.0 2.4 %fusion.7 = bf16[1,1,96,4096]{3,2,1,0:T(8,128)(2,1)} fusion(bf16[1,1,96,4096]{3,2,1,0:T(8,128)(2,1)} %param.10, f32[1,1,96,4096]{3,2,1,0:T(8,128)S(1)} %reshape.131, f32[4096]{0:T(1024)S(1)} %bitcast.59, f32[96]{0:T(128)S(1)} %add_rsqrt_fusion, f32[]{:T(128)} %bitcast), kind=kLoop, calls=%fused_computation.13 | loop fusion | flops 2359296 | bytes 3162500 | tf_op jit(solution)/shard_map/convert_element_type | solution.py:76
  144.4 13.1 %collective-permute-done = bf16[96,4096]{1,0:T(8,128)(2,1)} collective-permute-done((bf16[96,4096]{1,0:T(8,128)(2,1)}, bf16[96,4096]{1,0:T(8,128)(2,1)}, u32[]{:S(2)}, u32[]{:S(2)}) %collective-permute-start) | collective-permute-done | bytes 786464 | tf_op jit(solution)/shard_map/ppermute | solution.py:21
  157.5 2.1 %select_bitcast_fusion = bf16[1,1,96,4096]{3,2,1,0:T(8,128)(2,1)} fusion(bf16[96,4096]{1,0:T(8,128)(2,1)} %collective-permute-done, bf16[96,4096]{1,0:T(8,128)(2,1)} %fusion.9, pred[]{:T(512)} %bitcast.13), kind=kLoop, calls=%fused_computation.25 | loop fusion | flops 393216 | bytes 2359297 | tf_op jit(solution)/shard_map/broadcast_in_dim | solution.py:80
  (22 shorter events, 11.1 us)
Async XLA Ops:
  6.3 29.9 %all-to-all-start = ((bf16[2,96,4096]{1,0,2:T(2,128)(2,1)}), bf16[2,96,4096]{1,0,2:T(2,128)(2,1)S(1)}, u32[]{:S(2)}, u32[]{:S(2)}) async-start(bf16[2,96,4096]{1,0,2:T(2,128)(2,1)} %bitcast.50), calls=%async_computation | async-start | bytes 4194304 | tf_op jit(solution)/shard_map/all_to_all | solution.py:61
  36.3 30.2 %all-to-all-start.1 = ((bf16[2,96,4096]{1,0,2:T(2,128)(2,1)}), bf16[2,96,4096]{1,0,2:T(2,128)(2,1)}, u32[]{:S(2)}, u32[]{:S(2)}) async-start(bf16[2,96,4096]{1,0,2:T(2,128)(2,1)} %bitcast.49), calls=%async_computation.1 | async-start | bytes 4194304 | tf_op jit(solution)/shard_map/all_to_all | solution.py:62
  66.4 30.2 %all-to-all-start.2 = ((bf16[2,96,4096]{1,0,2:T(2,128)(2,1)}), bf16[2,96,4096]{1,0,2:T(2,128)(2,1)}, u32[]{:S(2)}, u32[]{:S(2)}) async-start(bf16[2,96,4096]{1,0,2:T(2,128)(2,1)} %bitcast.48), calls=%async_computation.2 | async-start | bytes 4194304 | tf_op jit(solution)/shard_map/all_to_all | solution.py:63
  83.0 3.6 %copy-start = (f32[2,8,384,384]{2,3,1,0:T(8,128)}, f32[2,8,384,384]{2,3,1,0:T(8,128)S(1)}, u32[]{:S(2)}) copy-start(f32[2,8,384,384]{2,3,1,0:T(8,128)S(1)} %fusion.12) | copy-start | bytes 28311556
  115.1 1.9 %copy-start.1 = (f32[4,96,1024]{2,1,0:T(8,128)S(1)}, f32[4,96,1024]{2,1,0:T(8,128)}, u32[]{:S(2)}) copy-start(f32[4,96,1024]{2,1,0:T(8,128)} %reshape.129) | copy-start | bytes 4718596
  119.7 4.5 %copy-start.3 = (bf16[1,4096]{1,0:T(2,128)(2,1)S(1)}, bf16[1,4096]{1,0:T(2,128)(2,1)}, u32[]{:S(2)}) copy-start(bf16[1,4096]{1,0:T(2,128)(2,1)} %param.11) | copy-start | bytes 24580
  119.7 15.2 %all-to-all-start.3 = ((bf16[4,96,1024]{2,1,0:T(8,128)(2,1)}), bf16[4,96,1024]{2,1,0:T(8,128)(2,1)S(1)}, u32[]{:S(2)}, u32[]{:S(2)}) async-start(bf16[4,96,1024]{2,1,0:T(8,128)(2,1)} %add_convert_fusion), calls=%async_computation.3 | async-start | bytes 1572864 | tf_op jit(solution)/shard_map/all_to_all | solution.py:66
  135.3 1.1 copy-start.2
  137.7 19.8 %collective-permute-start = (bf16[96,4096]{1,0:T(8,128)(2,1)}, bf16[96,4096]{1,0:T(8,128)(2,1)}, u32[]{:S(2)}, u32[]{:S(2)}) collective-permute-start(bf16[96,4096]{1,0:T(8,128)(2,1)} %fusion.9), channel_id=1, source_target_pairs={{0,16},{16,0},{1,17},{17,1},{2,18},{18,2},{3,19},{19,3},{4,20},{20... | collective-permute-start | bytes 2359304 | tf_op jit(solution)/shard_map/ppermute | solution.py:21
where the time goes:
time: 161 us; the launch traced here: 160 us
  waiting for transfers between devices  70.7 us (44%)
  local copies, waits for them, and re-layouts  44.6 us (28%)
  starting transfers between devices  19.2 us (12%)
  other arithmetic  11.6 us (7%)
  matrix products  11.3 us (7%)
  between operations  2.2 us (1%)
    unnamed x14, local copies, waits for them, and re-layouts  24.7 us
    all_to_all x1, waiting for transfers between devices, per_device(): lax.all_to_all(keys[0, 0], 'seq', split_axis=2, concat_axis=1, tiled=True)  20 us
    all_to_all x1, waiting for transfers between devices, per_device(): lax.all_to_all(queries[0, 0], 'seq', split_axis=2, concat_axis=1, tiled=T...  20 us
    ppermute x1, waiting for transfers between devices, from_partner(): return lax.ppermute(block, axis, route)  13.1 us
    all_to_all x1, waiting for transfers between devices, per_device(): lax.all_to_all(combine(attended[0], attended[1]), 'seq', split_axis=0, co...  9.97 us
    dot_general x1, matrix products, one_block(): jnp.einsum('nhqk,nkhd->nqhd', weights, value_rows, preferred_element_type...  9.9 us
    all_to_all x1, waiting for transfers between devices, per_device(): lax.all_to_all(values[0, 0], 'seq', split_axis=2, concat_axis=1, tiled=True)  7.6 us
    all_to_all x1, local copies, waits for them, and re-layouts, per_device(): lax.all_to_all(keys[0, 0], 'seq', split_axis=2, concat_axis=1, tiled=True)  4.67 us
  transfers between devices with their start and end apart: 5, of which 5 were waited for; matrix products, arithmetic and copies ran while one was open for 19% of the time, Pallas kernels for 0%

commit v1 on v0

--- a/solution.py
+++ b/solution.py
@@ -1,6 +1,10 @@
+import functools
+
 import jax
 import jax.numpy as jnp
 from jax import lax
+from jax.experimental import pallas as pl
+from jax.experimental.pallas import tpu as pltpu
 from jax.sharding import PartitionSpec as P
 
 HDIM = 128
@@ -55,7 +59,7 @@
     return result.transpose(1, 0, 2, 3, 4).reshape(items, length, width_dev)
 
 
-def per_device(queries, keys, values, latents, gain, steps_table, flags):
+def exchange_heads(queries, keys, values, latents, gain, steps_table, flags):
     attended = attend(
         (
             lax.all_to_all(queries[0, 0], "seq", split_axis=2, concat_axis=1, tiled=True),
@@ -80,6 +84,262 @@
     return (denoised[None, None], next_latents[None, None])
 
 
+MESH = pl.DeviceIdType.MESH
+HEADS_AT_ONCE = 2
+PIECE = 16
+
+
+def head_cols(head):
+    return pl.ds(pl.multiple_of(head * HDIM, HDIM), HDIM)
+
+
+def partial_attention(query, key_rows, value_rows):
+    scores = lax.dot_general(
+        query, key_rows, (((1,), (1,)), ((), ())), preferred_element_type=jnp.float32
+    )
+    top = jnp.max(scores, axis=-1, keepdims=True)
+    powers = jnp.exp((scores - top) * HDIM ** (-0.5))
+    total = jnp.sum(powers, axis=-1, keepdims=True)
+    part = jnp.dot(powers.astype(jnp.bfloat16), value_rows, preferred_element_type=jnp.float32)
+    return part / total, top * HDIM ** (-0.5) + jnp.log(total)
+
+
+def share(mine, other):
+    return 1.0 / (1.0 + jnp.exp(other - mine))
+
+
+def pair_kernel(
+    queries, keys, values, latents, gain, steps,
+    denoised, moved, partner,
+    q_own, q_far, k_all, v_all, part_own, part_far, part_back, current, den_rows, mov_rows,
+    guided, lse_own, lse_peer, lse_far, lse_back, gain_now, gain_move,
+    load_sems, kv_sems, q_sems, lse_sems, back_sems, back_lse_sems, cross_sems, store_sems,
+):
+    seq = lax.axis_index("seq")
+    size = lax.axis_size("seq")
+    beside = {"seq": seq + 1 - 2 * lax.rem(seq, 2)}
+    across = {"seq": lax.rem(seq + size // 2, size)}
+    other = {"expert": 1 - lax.axis_index("expert")}
+    branches, rows, width = queries.shape
+    heads = width // HDIM
+    half = rows // 2
+    pieces = rows // PIECE
+
+    own_keys = pl.ds(0, rows)
+    loads = [
+        pltpu.make_async_copy(queries, q_own, load_sems.at[0]),
+        pltpu.make_async_copy(keys, k_all.at[:, own_keys], load_sems.at[1]),
+        pltpu.make_async_copy(values, v_all.at[:, own_keys], load_sems.at[2]),
+        pltpu.make_async_copy(latents, current, load_sems.at[3]),
+    ]
+    for load in loads:
+        load.start()
+
+    barrier = pltpu.get_barrier_semaphore()
+    for peer in (beside, across, other):
+        pl.semaphore_signal(barrier, inc=1, device_id=peer, device_id_type=MESH)
+    pl.semaphore_wait(barrier, 3)
+
+    def remote(source, target, sems, index, peer):
+        return pltpu.make_async_remote_copy(
+            src_ref=source, dst_ref=target, send_sem=sems.at[0, index],
+            recv_sem=sems.at[1, index], device_id=peer, device_id_type=MESH,
+        )
+
+    q_sends = [
+        remote(queries.at[:, pl.ds(at * half, half)], q_far.at[:, pl.ds(at * half, half)],
+               q_sems, at, across)
+        for at in range(2)
+    ]
+    q_sends[0].start()
+    peer_keys = pl.ds(rows, rows)
+    kv_sends = [
+        remote(keys, k_all.at[:, peer_keys], kv_sems, 0, beside),
+        remote(values, v_all.at[:, peer_keys], kv_sems, 1, beside),
+    ]
+    for send in kv_sends:
+        send.start()
+
+    step = jnp.full((1, HDIM), steps[0, 0], jnp.int32)
+    sigma_now = sigma_of(step)[:, :1]
+    sigma_next = sigma_of(step + 1)[:, :1]
+    row = gain[...].astype(jnp.float32)
+    gain_now[...] = sigma_now * row
+    gain_move[...] = (sigma_next - sigma_now) * row
+
+    for load in loads:
+        load.wait()
+    for send in kv_sends:
+        send.wait_recv()
+
+    lane = lax.broadcasted_iota(jnp.int32, (1, HDIM), 1)
+
+    def own_heads(step_at, lse):
+        for extra in range(HEADS_AT_ONCE):
+            head = step_at * HEADS_AT_ONCE + extra
+            cols = head_cols(head)
+            for branch in range(branches):
+                part, stat = partial_attention(
+                    q_own[branch, :, cols], k_all[branch, :, cols], v_all[branch, :, cols]
+                )
+                part_own[branch, :, cols] = part
+                lse = jnp.where(lane == branch * heads + head, stat, lse)
+        return lse
+
+    lse_own[...] = lax.fori_loop(
+        0, heads // HEADS_AT_ONCE, own_heads, jnp.zeros((rows, HDIM), jnp.float32)
+    )
+    lse_send = remote(lse_own, lse_peer, lse_sems, 0, across)
+    lse_send.start()
+    q_sends[1].start()
+    lse_send.wait_recv()
+
+    def back_copies(piece):
+        at = pl.ds(pl.multiple_of(piece * PIECE, PIECE), PIECE)
+        return (
+            remote(lse_far.at[at], lse_back.at[at], back_lse_sems, piece, across),
+            remote(part_far.at[at], part_back.at[at], back_sems, piece, across),
+        )
+
+    for at in range(2):
+        q_sends[at].wait_recv()
+        here = pl.ds(at * half, half)
+        peer_lse = lse_peer[here, :]
+
+        def far_heads(step_at, lse):
+            for extra in range(HEADS_AT_ONCE):
+                head = step_at * HEADS_AT_ONCE + extra
+                cols = head_cols(head)
+                terms = []
+                for branch in range(branches):
+                    part, stat = partial_attention(
+                        q_far[branch, here, cols], k_all[branch, :, cols], v_all[branch, :, cols]
+                    )
+                    spot = lane == branch * heads + head
+                    lse = jnp.where(spot, stat, lse)
+                    theirs = jnp.sum(jnp.where(spot, peer_lse, 0.0), axis=-1, keepdims=True)
+                    terms.append(part * share(stat, theirs))
+                part_far[here, cols] = (GUIDANCE * terms[0] + (1.0 - GUIDANCE) * terms[1]).astype(
+                    jnp.bfloat16
+                )
+            return lse
+
+        lse_far[here, :] = lax.fori_loop(
+            0, heads // HEADS_AT_ONCE, far_heads, jnp.zeros((half, HDIM), jnp.float32)
+        )
+        for piece in range(at * pieces // 2, (at + 1) * pieces // 2):
+            for copy in back_copies(piece):
+                copy.start()
+
+    def result_copies(piece):
+        at = pl.ds(pl.multiple_of(piece * PIECE, PIECE), PIECE)
+        return (
+            remote(mov_rows.at[at], partner.at[at], cross_sems, piece, other),
+            pltpu.make_async_copy(den_rows.at[at], denoised.at[at], store_sems.at[0, piece]),
+            pltpu.make_async_copy(mov_rows.at[at], moved.at[at], store_sems.at[1, piece]),
+        )
+
+    def finish(piece, carry):
+        at = pl.ds(pl.multiple_of(piece * PIECE, PIECE), PIECE)
+        for copy in back_copies(piece):
+            copy.wait_recv()
+        weight = share(lse_own[at, :], lse_back[at, :])
+        squares = jnp.zeros((PIECE, HDIM), jnp.float32)
+        for head in range(heads):
+            cols = pl.ds(head * HDIM, HDIM)
+            uncond = heads + head
+            value = (
+                GUIDANCE * weight[:, head : head + 1] * part_own[0, at, cols]
+                + (1.0 - GUIDANCE) * weight[:, uncond : uncond + 1] * part_own[1, at, cols]
+                + part_back[at, cols].astype(jnp.float32)
+            ).astype(jnp.bfloat16).astype(jnp.float32)
+            guided[:, cols] = value
+            squares += value * value
+        mean = jnp.sum(squares, axis=-1, keepdims=True) / width
+        scale = lax.rsqrt(mean + 1e-06)
+        for head in range(heads):
+            cols = pl.ds(head * HDIM, HDIM)
+            unit = guided[:, cols] * scale
+            now = current[at, cols].astype(jnp.float32)
+            mov_rows[at, cols] = (now + gain_move[:, cols] * unit).astype(jnp.bfloat16)
+            den_rows[at, cols] = (now - gain_now[:, cols] * unit).astype(jnp.bfloat16)
+        for copy in result_copies(piece):
+            copy.start()
+        return carry
+
+    lax.fori_loop(0, pieces, finish, 0)
+
+    for send in q_sends + kv_sends + [lse_send]:
+        send.wait_send()
+
+    def drain(piece, carry):
+        for copy in back_copies(piece):
+            copy.wait_send()
+        for copy in result_copies(piece):
+            copy.wait()
+        return carry
+
+    lax.fori_loop(0, pieces, drain, 0)
+
+
+def exchange_queries(queries, keys, values, latents, gain, steps_table, flags):
+    branches, rows, width = queries.shape[2:]
+    pieces = rows // PIECE
+    whole = jax.ShapeDtypeStruct((rows, width), jnp.bfloat16)
+    hbm = pl.BlockSpec(memory_space=pltpu.HBM)
+    low = functools.partial(pltpu.VMEM, dtype=jnp.bfloat16)
+    high = functools.partial(pltpu.VMEM, dtype=jnp.float32)
+    dma = pltpu.SemaphoreType.DMA
+    denoised, moved, partner = pl.pallas_call(
+        pair_kernel,
+        out_shape=(whole, whole, whole),
+        in_specs=[hbm] * 4
+        + [pl.BlockSpec(memory_space=pltpu.VMEM), pl.BlockSpec(memory_space=pltpu.SMEM)],
+        out_specs=(hbm, hbm, hbm),
+        scratch_shapes=[
+            low((branches, rows, width)),
+            low((branches, rows, width)),
+            low((branches, 2 * rows, width)),
+            low((branches, 2 * rows, width)),
+            high((branches, rows, width)),
+            low((rows, width)),
+            low((rows, width)),
+            low((rows, width)),
+            low((rows, width)),
+            low((rows, width)),
+            high((PIECE, width)),
+            high((rows, HDIM)),
+            high((rows, HDIM)),
+            high((rows, HDIM)),
+            high((rows, HDIM)),
+            high((1, width)),
+            high((1, width)),
+            dma((4,)),
+            dma((2, 2)),
+            dma((2, 2)),
+            dma((2, 1)),
+            dma((2, pieces)),
+            dma((2, pieces)),
+            dma((2, pieces)),
+            dma((2, pieces)),
+        ],
+        compiler_params=pltpu.CompilerParams(collective_id=0, has_side_effects=True),
+    )(queries[0, 0], keys[0, 0], values[0, 0], latents[0, 0], gain, steps_table)
+    next_latents = jnp.where(flags[0] == 1, partner, moved)
+    return (denoised[None, None], next_latents[None, None])
+
+
+def per_device(*blocks):
+    branches, rows, width = blocks[0].shape[2:]
+    paired = (
+        lax.axis_size("seq") == 2 * 2
+        and lax.axis_size("expert") == 2
+        and rows % (2 * PIECE) == 0
+        and branches * width // HDIM <= HDIM
+    )
+    return (exchange_queries if paired else exchange_heads)(*blocks)
+
+
 def solution(mesh):
     placed = (
         P("expert", "batch", None, "seq", None),

time: 161 us -> 93 us (0.58)
  Pallas kernels: 0 us -> 87.7 us
  waiting for transfers between devices: 70.7 us -> 0 us
  local copies, waits for them, and re-layouts: 44.6 us -> 0.88 us
  starting transfers between devices: 19.2 us -> 0 us
  matrix products: 11.3 us -> 0 us
  other arithmetic: 11.6 us -> 2.18 us
    pallas_call x0 -> x1, Pallas kernels: none -> 87.7 us  [exchange_queries(): pl.pallas_call(pair_kernel, out_shape=(whole, whole, whole), in_specs=[hb...]
    all_to_all x4 -> x0, waiting for transfers between devices: 57.6 us -> none  [the longest x1 20 us: per_device(): lax.all_to_all(keys[0, 0], 'seq', split_axis=2, concat_axis=1, tiled=True)]
    unnamed x14 -> x3, local copies, waits for them, and re-layouts: 24.7 us -> 0.88 us
    all_to_all x4 -> x0, starting transfers between devices: 16.9 us -> none  [the longest x1 4.44 us: per_device(): lax.all_to_all(keys[0, 0], 'seq', split_axis=2, concat_axis=1, tiled=True)]
    ppermute x1 -> x0, waiting for transfers between devices: 13.1 us -> none  [from_partner(): return lax.ppermute(block, axis, route)]
    all_to_all x3 -> x0, local copies, waits for them, and re-layouts: 13 us -> none  [the longest x1 4.67 us: per_device(): lax.all_to_all(keys[0, 0], 'seq', split_axis=2, concat_axis=1, tiled=True)]
    dot_general x2 -> x0, matrix products: 11.3 us -> none  [the longest x1 9.9 us: one_block(): jnp.einsum('nhqk,nkhd->nqhd', weights, value_rows, preferred_element_type...]
    convert_element_type x7 -> x0, local copies, waits for them, and re-layouts: 6.82 us -> none  [the longest x2 2.32 us: combine(): base = uncond.astype(jnp.float32)]
  transfers between devices with their start and end apart: 5 -> 0, of which waited for: 5 -> 0; matrix products, arithmetic and copies ran while one was open for 19% -> 0% of each run, Pallas kernels for 0% -> 0%
where the time goes in v1:
time: 93 us; the launch traced here: 92.7 us
  Pallas kernels  87.7 us (94%)
  other arithmetic  2.18 us (2%)
  between operations  1.94 us (2%)
    pallas_call x1, Pallas kernels, exchange_queries(): pl.pallas_call(pair_kernel, out_shape=(whole, whole, whole), in_specs=[hb...  87.7 us
    broadcast_in_dim x1, other arithmetic, exchange_queries(): return (denoised[None, None], next_latents[None, None])  2.18 us

profile of v1, /device:TPU:0, one launch (start us, length us, event | category | flops | bytes accessed | tf_op | source)
XLA Modules:
  0.0 92.7 jit_solution(270796288455219791)
XLA Ops:
  1.9 87.7 %shard_map.86 = (bf16[96,4096]{1,0:T(8,128)(2,1)}, bf16[96,4096]{1,0:T(8,128)(2,1)}, bf16[96,4096]{1,0:T(8,128)(2,1)}) custom-call(bf16[2,96,4096]{2,1,0:T(8,128)(2,1)} %bitcast.8, bf16[2,96,4096]{2,1,0:T(8,128)(2,1)} %bitcast.9, bf16[2,96,4096]{2,1,0:T(8,128)(2,1)} %bitcast.10, bf16[96,4096]{1,0:T(8,128)(2,1)} %bitcast.12, bf16[1,4096]{1,0:T(2,128)(2,1)} %gain.1, ...), custom_call_target="tpu_custom_call" | custom-call | tf_op jit(solution)/shard_map/pallas_call | solution.py:293
  89.6 0.0 copy-start
  89.6 2.2 %select_bitcast_fusion = bf16[1,1,96,4096]{3,2,1,0:T(8,128)(2,1)} fusion(bf16[96,4096]{1,0:T(8,128)(2,1)} %get-tuple-element.6, bf16[96,4096]{1,0:T(8,128)(2,1)} %get-tuple-element.7, pred[]{:T(512)} %bitcast.5), kind=kLoop, calls=%fused_computation | loop fusion | flops 393216 | bytes 2359297 | tf_op jit(solution)/shard_map/broadcast_in_dim | solution.py:329
  91.8 0.0 copy-done
  91.8 0.9 copy.12
Async XLA Ops:
  89.6 2.2 %copy-start = (bf16[96,4096]{1,0:T(8,128)(2,1)S(1)}, bf16[96,4096]{1,0:T(8,128)(2,1)}, u32[]{:S(2)}) copy-start(bf16[96,4096]{1,0:T(8,128)(2,1)} %get-tuple-element.5) | copy-start | bytes 2359300

commit v2 on v1

--- a/solution.py
+++ b/solution.py
@@ -85,8 +85,9 @@
 
 
 MESH = pl.DeviceIdType.MESH
-HEADS_AT_ONCE = 2
+HEADS_AT_ONCE = 4
 PIECE = 16
+LATE = 2
 
 
 def head_cols(head):
@@ -147,17 +148,18 @@
         )
 
     q_sends = [
-        remote(queries.at[:, pl.ds(at * half, half)], q_far.at[:, pl.ds(at * half, half)],
+        remote(queries.at[:, pl.ds(at * PIECE, PIECE)], q_far.at[:, pl.ds(at * PIECE, PIECE)],
                q_sems, at, across)
-        for at in range(2)
+        for at in range(pieces)
     ]
-    q_sends[0].start()
     peer_keys = pl.ds(rows, rows)
     kv_sends = [
         remote(keys, k_all.at[:, peer_keys], kv_sems, 0, beside),
         remote(values, v_all.at[:, peer_keys], kv_sems, 1, beside),
     ]
     for send in kv_sends:
+        send.start()
+    for send in q_sends[:-LATE]:
         send.start()
 
     step = jnp.full((1, HDIM), steps[0, 0], jnp.int32)
@@ -191,7 +193,8 @@
     )
     lse_send = remote(lse_own, lse_peer, lse_sems, 0, across)
     lse_send.start()
-    q_sends[1].start()
+    for send in q_sends[-LATE:]:
+        send.start()
     lse_send.wait_recv()
 
     def back_copies(piece):
@@ -202,7 +205,8 @@
         )
 
     for at in range(2):
-        q_sends[at].wait_recv()
+        for send in q_sends[at * pieces // 2 : (at + 1) * pieces // 2]:
+            send.wait_recv()
         here = pl.ds(at * half, half)
         peer_lse = lse_peer[here, :]
 
@@ -316,7 +320,7 @@
             high((1, width)),
             dma((4,)),
             dma((2, 2)),
-            dma((2, 2)),
+            dma((2, pieces)),
             dma((2, 1)),
             dma((2, pieces)),
             dma((2, pieces)),

time: 93 us -> 89.8 us (0.966)
  Pallas kernels: 87.7 us -> 84.5 us
    pallas_call x1, Pallas kernels: 87.7 us -> 84.5 us  [exchange_queries(): pl.pallas_call(pair_kernel, out_shape=(whole, whole, whole), in_specs=[hb...]
where the time goes in v2:
time: 89.8 us; the launch traced here: 89.5 us
  Pallas kernels  84.5 us (94%)
  other arithmetic  2.18 us (2%)
  between operations  1.94 us (2%)
    pallas_call x1, Pallas kernels, exchange_queries(): pl.pallas_call(pair_kernel, out_shape=(whole, whole, whole), in_specs=[hb...  84.5 us
    broadcast_in_dim x1, other arithmetic, exchange_queries(): return (denoised[None, None], next_latents[None, None])  2.18 us

profile of v2, /device:TPU:0, one launch (start us, length us, event | category | flops | bytes accessed | tf_op | source)
XLA Modules:
  0.0 89.5 jit_solution(9070299570204854354)
XLA Ops:
  1.9 84.5 %shard_map.86 = (bf16[96,4096]{1,0:T(8,128)(2,1)}, bf16[96,4096]{1,0:T(8,128)(2,1)}, bf16[96,4096]{1,0:T(8,128)(2,1)}) custom-call(bf16[2,96,4096]{2,1,0:T(8,128)(2,1)} %bitcast.8, bf16[2,96,4096]{2,1,0:T(8,128)(2,1)} %bitcast.9, bf16[2,96,4096]{2,1,0:T(8,128)(2,1)} %bitcast.10, bf16[96,4096]{1,0:T(8,128)(2,1)} %bitcast.12, bf16[1,4096]{1,0:T(2,128)(2,1)} %gain.1, ...), custom_call_target="tpu_custom_call" | custom-call | tf_op jit(solution)/shard_map/pallas_call | solution.py:297
  86.5 0.0 copy-start
  86.5 2.2 %select_bitcast_fusion = bf16[1,1,96,4096]{3,2,1,0:T(8,128)(2,1)} fusion(bf16[96,4096]{1,0:T(8,128)(2,1)} %get-tuple-element.6, bf16[96,4096]{1,0:T(8,128)(2,1)} %get-tuple-element.7, pred[]{:T(512)} %bitcast.5), kind=kLoop, calls=%fused_computation | loop fusion | flops 393216 | bytes 2359297 | tf_op jit(solution)/shard_map/broadcast_in_dim | solution.py:333
  88.7 0.0 copy-done
  88.7 0.9 copy.12
Async XLA Ops:
  86.5 2.2 %copy-start = (bf16[96,4096]{1,0:T(8,128)(2,1)S(1)}, bf16[96,4096]{1,0:T(8,128)(2,1)}, u32[]{:S(2)}) copy-start(bf16[96,4096]{1,0:T(8,128)(2,1)} %get-tuple-element.5) | copy-start | bytes 2359300
